TPU v7x, 32 devices: a whole 2x2x4 slice. The times are simulated.
32 devices in a mesh: dp: 4 (over x, core), seq: 8 (over z, y).
Axes of the slice: x: 2, y: 2, z: 4, core: 2. Of those that a mesh axis runs over, the one named last changes fastest.
Arguments:
- tokens: bfloat16 [8, 1152, 1280], P('dp', 'seq'), may hold values from -60 to 60
- pre_gain: float32 [1280], replicated, may hold values from 0.5 to 1.5
- pre_shift: float32 [1280], replicated, may hold values from -3 to 3
- w_qkv: bfloat16 [1280, 3840], P('dp'), may hold values from -4 to 4
- qkv_bias: float32 [3840], replicated, may hold values from -3 to 3
- w_out: bfloat16 [1280, 1280], P('dp'), may hold values from -0.15625 to 0.15625
- out_bias: float32 [1280], replicated, may hold values from -3 to 3
- mlp_gain: float32 [1280], replicated, may hold values from 0.5 to 1.5
- mlp_shift: float32 [1280], replicated, may hold values from -3 to 3
- w_up: bfloat16 [1280, 2560], P('dp'), may hold values from -0.15625 to 0.15625
- up_bias: float32 [2560], replicated, may hold values from -3 to 3
- w_down: bfloat16 [2560, 1280], P('dp'), may hold values from -0.125 to 0.125
- down_bias: float32 [1280], replicated, may hold values from -3 to 3
Outputs:
- layer_out: bfloat16 [8, 1152, 1280], P('dp', 'seq')
All inputs are finite; a program needn't handle non-finite values.
Results may differ from a plain program's by a relative error of at most 0.0039.
Values may be sent and summed in bfloat16 or wider, within the bound.
A program may use at most 128 MiB of HBM per device.

v0:
```python
import math

import jax
import jax.numpy as jnp
from jax import lax
from jax.sharding import PartitionSpec as P

HEADS = 16
HEAD_DIM = 80


EPSILON = 1e-05


def normalize(features, gain, shift):
    average = jnp.mean(features, axis=-1, keepdims=True)
    centered = features - average
    spread = jnp.mean(centered * centered, axis=-1, keepdims=True)
    return centered * lax.rsqrt(spread + EPSILON) * gain + shift


def fold_rows(left_side, shard_piece):
    return jnp.dot(left_side, shard_piece, preferred_element_type=jnp.float32)


def query_block(length):
    block_rows = length
    while block_rows > 1024 and block_rows % 2 == 0:
        block_rows = block_rows // 2
    return block_rows


def attend_back(packed_items):
    count, length, heads_here, triple = packed_items.shape
    head_size = triple // 3
    block_rows = query_block(length)
    factor = 1.0 / math.sqrt(head_size)

    def one_picture(picture):
        key_rows = picture[:, :, head_size : 2 * head_size]
        value_rows = picture[:, :, 2 * head_size :]
        queries = picture[:, :, :head_size].reshape(
            length // block_rows, block_rows, heads_here, head_size
        )

        def one_block(query_rows):
            scores = (
                jnp.einsum("qhd,khd->hqk", query_rows, key_rows, preferred_element_type=jnp.float32)
                * factor
            )
            highest = jnp.max(scores, axis=-1, keepdims=True)
            weights = jnp.exp(scores - highest)
            probs = (weights / jnp.sum(weights, axis=-1, keepdims=True)).astype(jnp.bfloat16)
            mixed = jnp.einsum(
                "hqk,khd->qhd", probs, value_rows, preferred_element_type=jnp.float32
            )
            return mixed.astype(jnp.bfloat16)

        outputs = lax.map(one_block, queries)
        return outputs.reshape(length, heads_here * head_size)

    context = lax.map(one_picture, packed_items)
    return lax.all_to_all(context, "seq", split_axis=1, concat_axis=2, tiled=True)


def shards(
    tokens,
    pre_gain,
    pre_shift,
    w_qkv,
    qkv_bias,
    w_out,
    out_bias,
    mlp_gain,
    mlp_shift,
    w_up,
    up_bias,
    w_down,
    down_bias,
):
    images_here, tok_here, width = tokens.shape
    row_count = images_here * tok_here
    triple = 3 * HEAD_DIM
    residual = tokens.reshape(row_count, width).astype(jnp.float32)
    normed = normalize(residual, pre_gain, pre_shift).astype(jnp.bfloat16)
    projected = fold_rows(normed, lax.all_gather(w_qkv, "dp", axis=0, tiled=True))
    packed = (
        (projected + qkv_bias).astype(jnp.bfloat16).reshape(images_here, tok_here, HEADS, triple)
    )
    context = attend_back(lax.all_to_all(packed, "seq", split_axis=2, concat_axis=1, tiled=True))
    context = context.reshape(row_count, width)
    attended = fold_rows(context, lax.all_gather(w_out, "dp", axis=0, tiled=True))
    middle = residual + attended + out_bias
    normed_mlp = normalize(middle, mlp_gain, mlp_shift).astype(jnp.bfloat16)
    lifted = fold_rows(normed_mlp, lax.all_gather(w_up, "dp", axis=0, tiled=True))
    hidden = jax.nn.gelu(lifted + up_bias, approximate=False).astype(jnp.bfloat16)
    lowered = fold_rows(hidden, lax.all_gather(w_down, "dp", axis=0, tiled=True))
    result = (middle + lowered + down_bias).astype(jnp.bfloat16)
    return result.reshape(images_here, tok_here, width)


def solution(mesh):
    in_specs = (
        P("dp", "seq", None),
        P(),
        P(),
        P("dp", None),
        P(),
        P("dp", None),
        P(),
        P(),
        P(),
        P("dp", None),
        P(),
        P("dp", None),
        P(),
    )
    out_specs = P("dp", "seq", None)
    return jax.shard_map(shards, mesh=mesh, in_specs=in_specs, out_specs=out_specs, check_vma=False)
```

profile of v0, /device:TPU:0, one launch (start us, length us, event | category | flops | bytes accessed | tf_op | source)
XLA Modules:
  0.0 254.2 jit_solution(1790984664754950806)
XLA Ops:
  9.8 68.2 %all-gather.5.cloned.1.call-done = bf16[1280,3840]{1,0:T(8,128)(2,1)} async-done(((bf16[320,3840]{1,0:T(8,128)(2,1)}), bf16[1280,3840]{1,0:T(8,128)(2,1)}) %all-gather.5.cloned.1.call-update) | async-done | bytes 9830416 | tf_op jit(solution)/shard_map/all_gather | solution.py:86
  78.1 8.1 %fusion.31 = bf16[288,3840]{1,0:T(8,128)(2,1)} fusion(bf16[288,1280]{1,0:T(8,128)(2,1)S(1)} %fusion.48, bf16[1280,3840]{1,0:T(8,128)(2,1)} %all-gather.5.cloned.1.call-done, f32[3840]{0:T(1024)S(1)} %copy-done.4), kind=kOutput, calls=%fused_computation.25 | convolution fusion | flops 2833367040 | bytes 12794880 | tf_op jit(solution)/shard_map/dot_general | solution.py:23
  86.2 6.3 %reshape.72 = bf16[2,144,16,240]{3,2,1,0:T(8,128)(2,1)S(1)} reshape(bf16[288,3840]{1,0:T(8,128)(2,1)} %fusion.31) | data formatting | bytes 4423680 | tf_op jit(solution)/shard_map/reshape | solution.py:88
  92.5 2.3 copy.28
  94.8 5.5 %all-to-all-start = ((bf16[2,144,16,240]{3,1,0,2:T(8,128)(2,1)}), bf16[2,144,16,240]{3,1,0,2:T(8,128)(2,1)S(1)}, u32[]{:S(2)}, u32[]{:S(2)}) async-start(bf16[2,144,16,240]{3,1,0,2:T(8,128)(2,1)} %copy.28), calls=%async_computation | async-start | bytes 4718592 | tf_op jit(solution)/shard_map/all_to_all | solution.py:90
  100.9 53.7 %all-to-all-done = bf16[2,144,16,240]{3,1,0,2:T(8,128)(2,1)S(1)} async-done(((bf16[2,144,16,240]{3,1,0,2:T(8,128)(2,1)}), bf16[2,144,16,240]{3,1,0,2:T(8,128)(2,1)S(1)}, u32[]{:S(2)}, u32[]{:S(2)}) %all-to-all-start) | async-done | bytes 2211872 | tf_op jit(solution)/shard_map/all_to_all | solution.py:90
  154.6 1.7 copy.30
  156.3 3.0 %copy.31 = bf16[2,1152,2,240]{1,3,2,0:T(8,128)(2,1)S(1)} copy(bf16[2,1152,2,240]{3,1,2,0:T(8,128)(2,1)} %bitcast.73) | data formatting | bytes 4423680 | tf_op jit(solution)/shard_map/while | solution.py:62
  159.3 31.5 %while.21 = (s32[]{:T(128)}, bf16[2,1152,160]{1,2,0:T(8,128)(2,1)}, bf16[2,1152,2,240]{1,3,2,0:T(8,128)(2,1)S(1)}, s32[]{:T(128)}, s32[]{:T(128)}, /*index=5*/s32[]{:T(128)}) while((s32[]{:T(128)}, bf16[2,1152,160]{1,2,0:T(8,128)(2,1)}, bf16[2,1152,2,240]{1,3,2,0:T(8,128)(2,1)S(1)}, s32[]{:T(128)}, s32[]{:T(128)}, /*index=5*/s32[]{:T(128)}) %tuple.48), condition=%wide.region_7.8_spmd, body=%wide.region_2.7_spmd.sunk | while | flops 646395264 | bytes 9841866 | solution.py:62
  160.7 13.0 %while.22 = (s32[]{:T(128)}, bf16[2,576,2,80]{1,3,2,0:T(8,128)(2,1)S(1)}, bf16[2,576,2,80]{1,3,2,0:T(8,128)(2,1)S(1)}, bf16[1152,2,80]{0,2,1:T(8,128)(2,1)}, bf16[1152,2,80]{0,2,1:T(8,128)(2,1)S(1)}, /*index=5*/s32[]{:T(128)}) while((s32[]{:T(128)}, bf16[2,576,2,80]{1,3,2,0:T(8,128)(2,1)S(1)}, bf16[2,576,2,80]{1,3,2,0:T(8,128)(2,1)S(1)}, ...), condition=%wide.region_6.6_spmd, body=%wide.region_3.5_spmd.sunk | while | flops 646395264 | bytes 1731145 | solution.py:59
  160.7 2.9 %exponential_reduce_fusion.2 = f32[2,576]{1,0:T(2,128)S(1)} fusion(bf16[1152,2,80]{0,2,1:T(8,128)(2,1)} %get-tuple-element.179, bf16[2,576,2,80]{1,3,2,0:T(8,128)(2,1)S(1)} %get-tuple-element.178, s32[]{:T(128)} %get-tuple-element.170), kind=kOutput, calls=%fused_computation.4.clone.1 | convolution fusion | flops 216319104 | bytes 578052 | tf_op jit(solution)/shard_map/while/body/eval_jaxpr/while/body/eval_jaxpr/sub | solution.py:52
  163.6 3.5 %fusion.144 = bf16[2,576,2,80]{1,3,2,0:T(8,128)(2,1)S(1)} fusion(bf16[2,576,2,80]{1,3,2,0:T(8,128)(2,1)S(1)} %get-tuple-element.171, s32[]{:T(128)} %get-tuple-element.170, bf16[1152,2,80]{0,2,1:T(8,128)(2,1)S(1)} %get-tuple-element.180, f32[2,576]{1,0:T(2,128)S(1)} %exponential_reduce_fusion.2, bf16[1152,2,80]{0,2,1:T(8,128)(2,1)} %get-tuple-element.179, ...), kind=kOutput, calls=%fused_computation.8.clone.1 | convolution fusion | flops 430076160 | bytes 1153024 | tf_op jit(solution)/shard_map/while/body/eval_jaxpr/while/body/eval_jaxpr/hqk,khd->qhd/dot_general | solution.py:54
  167.2 2.9 %exponential_reduce_fusion.2 = f32[2,576]{1,0:T(2,128)S(1)} fusion(bf16[1152,2,80]{0,2,1:T(8,128)(2,1)} %get-tuple-element.179, bf16[2,576,2,80]{1,3,2,0:T(8,128)(2,1)S(1)} %get-tuple-element.178, s32[]{:T(128)} %get-tuple-element.170), kind=kOutput, calls=%fused_computation.4.clone.1 | convolution fusion | flops 216319104 | bytes 578052 | tf_op jit(solution)/shard_map/while/body/eval_jaxpr/while/body/eval_jaxpr/sub | solution.py:52
  170.1 3.6 %fusion.144 = bf16[2,576,2,80]{1,3,2,0:T(8,128)(2,1)S(1)} fusion(bf16[2,576,2,80]{1,3,2,0:T(8,128)(2,1)S(1)} %get-tuple-element.171, s32[]{:T(128)} %get-tuple-element.170, bf16[1152,2,80]{0,2,1:T(8,128)(2,1)S(1)} %get-tuple-element.180, f32[2,576]{1,0:T(2,128)S(1)} %exponential_reduce_fusion.2, bf16[1152,2,80]{0,2,1:T(8,128)(2,1)} %get-tuple-element.179, ...), kind=kOutput, calls=%fused_computation.8.clone.1 | convolution fusion | flops 430076160 | bytes 1153024 | tf_op jit(solution)/shard_map/while/body/eval_jaxpr/while/body/eval_jaxpr/hqk,khd->qhd/dot_general | solution.py:54
  176.5 12.9 %while.22 = (s32[]{:T(128)}, bf16[2,576,2,80]{1,3,2,0:T(8,128)(2,1)S(1)}, bf16[2,576,2,80]{1,3,2,0:T(8,128)(2,1)S(1)}, bf16[1152,2,80]{0,2,1:T(8,128)(2,1)}, bf16[1152,2,80]{0,2,1:T(8,128)(2,1)S(1)}, /*index=5*/s32[]{:T(128)}) while((s32[]{:T(128)}, bf16[2,576,2,80]{1,3,2,0:T(8,128)(2,1)S(1)}, bf16[2,576,2,80]{1,3,2,0:T(8,128)(2,1)S(1)}, ...), condition=%wide.region_6.6_spmd, body=%wide.region_3.5_spmd.sunk | while | flops 646395264 | bytes 1731145 | solution.py:59
  176.5 2.9 %exponential_reduce_fusion.2 = f32[2,576]{1,0:T(2,128)S(1)} fusion(bf16[1152,2,80]{0,2,1:T(8,128)(2,1)} %get-tuple-element.179, bf16[2,576,2,80]{1,3,2,0:T(8,128)(2,1)S(1)} %get-tuple-element.178, s32[]{:T(128)} %get-tuple-element.170), kind=kOutput, calls=%fused_computation.4.clone.1 | convolution fusion | flops 216319104 | bytes 578052 | tf_op jit(solution)/shard_map/while/body/eval_jaxpr/while/body/eval_jaxpr/sub | solution.py:52
  179.4 3.5 %fusion.144 = bf16[2,576,2,80]{1,3,2,0:T(8,128)(2,1)S(1)} fusion(bf16[2,576,2,80]{1,3,2,0:T(8,128)(2,1)S(1)} %get-tuple-element.171, s32[]{:T(128)} %get-tuple-element.170, bf16[1152,2,80]{0,2,1:T(8,128)(2,1)S(1)} %get-tuple-element.180, f32[2,576]{1,0:T(2,128)S(1)} %exponential_reduce_fusion.2, bf16[1152,2,80]{0,2,1:T(8,128)(2,1)} %get-tuple-element.179, ...), kind=kOutput, calls=%fused_computation.8.clone.1 | convolution fusion | flops 430076160 | bytes 1153024 | tf_op jit(solution)/shard_map/while/body/eval_jaxpr/while/body/eval_jaxpr/hqk,khd->qhd/dot_general | solution.py:54
  183.0 2.9 %exponential_reduce_fusion.2 = f32[2,576]{1,0:T(2,128)S(1)} fusion(bf16[1152,2,80]{0,2,1:T(8,128)(2,1)} %get-tuple-element.179, bf16[2,576,2,80]{1,3,2,0:T(8,128)(2,1)S(1)} %get-tuple-element.178, s32[]{:T(128)} %get-tuple-element.170), kind=kOutput, calls=%fused_computation.4.clone.1 | convolution fusion | flops 216319104 | bytes 578052 | tf_op jit(solution)/shard_map/while/body/eval_jaxpr/while/body/eval_jaxpr/sub | solution.py:52
  185.9 3.5 %fusion.144 = bf16[2,576,2,80]{1,3,2,0:T(8,128)(2,1)S(1)} fusion(bf16[2,576,2,80]{1,3,2,0:T(8,128)(2,1)S(1)} %get-tuple-element.171, s32[]{:T(128)} %get-tuple-element.170, bf16[1152,2,80]{0,2,1:T(8,128)(2,1)S(1)} %get-tuple-element.180, f32[2,576]{1,0:T(2,128)S(1)} %exponential_reduce_fusion.2, bf16[1152,2,80]{0,2,1:T(8,128)(2,1)} %get-tuple-element.179, ...), kind=kOutput, calls=%fused_computation.8.clone.1 | convolution fusion | flops 430076160 | bytes 1153024 | tf_op jit(solution)/shard_map/while/body/eval_jaxpr/while/body/eval_jaxpr/hqk,khd->qhd/dot_general | solution.py:54
  190.8 3.5 %copy.32 = bf16[2,1152,160]{2,0,1:T(2,128)(2,1)S(1)} copy(bf16[2,1152,160]{1,2,0:T(8,128)(2,1)} %get-tuple-element.49) | data formatting | bytes 1474560 | tf_op jit(solution)/shard_map/while | solution.py:62
  194.4 32.6 %all_to_all.33 = bf16[2,1152,160]{2,0,1:T(2,128)(2,1)S(1)} all-to-all(bf16[2,1152,160]{2,0,1:T(2,128)(2,1)S(1)} %copy.32), channel_id=1, replica_groups=mesh['dp'=4,'seq'=8] {'seq'}, dimensions={1} | all-to-all | bytes 1474560 | tf_op jit(solution)/shard_map/all_to_all | solution.py:63
  227.7 1.3 reshape.73
  229.1 3.2 %fusion.121 = (f32[288]{0:T(512)S(1)}, f32[288,1280]{1,0:T(8,128)S(1)}) fusion(f32[1280]{0:T(1024)S(1)} %copy-done.6, bf16[288,1280]{1,0:T(8,128)(2,1)S(1)} %reshape.73, bf16[1280,1280]{1,0:T(8,128)(2,1)} %all-gather.7.cloned.1.call-done, bf16[288,1280]{1,0:T(8,128)(2,1)S(1)} %bitcast.74), kind=kOutput, calls=%fused_computation.131 | convolution fusion | flops 945192704 | bytes 6232192 | tf_op jit(solution)/shard_map/dot_general | solution.py:23
  232.7 14.9 %fusion.44 = bf16[288,1280]{1,0:T(8,128)(2,1)} fusion(f32[288,1280]{1,0:T(8,128)S(1)} %get-tuple-element.94, bf16[2560,1280]{1,0:T(8,128)(2,1)} %all-gather.11.cloned.1.call-done, bf16[1280,2560]{1,0:T(8,128)(2,1)} %all-gather.9.cloned.1.call-done, f32[2560]{0:T(1024)S(1)} %copy-done.5, f32[1280]{0:T(1024)S(1)} %copy-done.7, f32[1280]{0:T(1024)S(1)} %copy-done.8, ...), kind=kOutput, calls=%fused_computation.50 | convolution fusion | flops 3826483200 | bytes 15346944 | tf_op jit(solution)/shard_map/dot_general | solution.py:23
  (59 shorter events, 10.4 us)
Async XLA Ops:
  6.5 2.2 copy-start
  6.5 2.9 %copy-start.2 = (f32[1280]{0:T(1024)S(1)}, f32[1280]{0:T(1024)}, u32[]{:S(2)}) copy-start(f32[1280]{0:T(1024)} %param.19) | copy-start | bytes 15364
  6.5 2.9 %copy-start.3 = (f32[1280]{0:T(1024)S(1)}, f32[1280]{0:T(1024)}, u32[]{:S(2)}) copy-start(f32[1280]{0:T(1024)} %param.18) | copy-start | bytes 15364
  6.5 71.6 %all-gather.5.cloned.1.call-start = ((), (), s32[]{:S(2)}) async-start(), calls=%async_computation.2 | async-start | bytes 12288000 | tf_op jit(solution)/shard_map/all_gather | solution.py:86
  7.3 70.8 %copy-start.4 = (f32[3840]{0:T(1024)S(1)}, f32[3840]{0:T(1024)}, u32[]{:S(2)}) copy-start(f32[3840]{0:T(1024)} %param.21) | copy-start | bytes 46084
  7.3 221.7 %all-gather.7.cloned.1.call-start = ((), (), s32[]{:S(2)}) async-start(), calls=%async_computation.3 | async-start | bytes 4096000 | tf_op jit(solution)/shard_map/all_gather | solution.py:92
  8.0 224.6 %all-gather.11.cloned.1.call-start = ((), (), s32[]{:S(2)}) async-start(), calls=%async_computation.5 | async-start | bytes 8192000 | tf_op jit(solution)/shard_map/all_gather | solution.py:97
  94.8 59.8 %all-to-all-start = ((bf16[2,144,16,240]{3,1,0,2:T(8,128)(2,1)}), bf16[2,144,16,240]{3,1,0,2:T(8,128)(2,1)S(1)}, u32[]{:S(2)}, u32[]{:S(2)}) async-start(bf16[2,144,16,240]{3,1,0,2:T(8,128)(2,1)} %copy.28), calls=%async_computation | async-start | bytes 4718592 | tf_op jit(solution)/shard_map/all_to_all | solution.py:90
  100.3 132.3 %all-gather.9.cloned.1.call-start = ((), (), s32[]{:S(2)}) async-start(), calls=%async_computation.4 | async-start | bytes 8192000 | tf_op jit(solution)/shard_map/all_gather | solution.py:95
  194.4 34.7 %copy-start.1 = (bf16[2,144,1280]{2,1,0:T(8,128)(2,1)S(1)}, bf16[2,144,1280]{2,1,0:T(8,128)(2,1)}, u32[]{:S(2)}) copy-start(bf16[2,144,1280]{2,1,0:T(8,128)(2,1)} %param.17) | copy-start | bytes 2211844
  194.4 34.7 %copy-start.6 = (f32[1280]{0:T(1024)S(1)}, f32[1280]{0:T(1024)}, u32[]{:S(2)}) copy-start(f32[1280]{0:T(1024)} %param.23) | copy-start | bytes 15364
  229.0 3.6 %copy-start.5 = (f32[2560]{0:T(1024)S(1)}, f32[2560]{0:T(1024)}, u32[]{:S(2)}) copy-start(f32[2560]{0:T(1024)} %param.27) | copy-start | bytes 30724
  229.0 3.6 %copy-start.7 = (f32[1280]{0:T(1024)S(1)}, f32[1280]{0:T(1024)}, u32[]{:S(2)}) copy-start(f32[1280]{0:T(1024)} %param.29) | copy-start | bytes 15364
  229.1 3.6 %copy-start.8 = (f32[1280]{0:T(1024)S(1)}, f32[1280]{0:T(1024)}, u32[]{:S(2)}) copy-start(f32[1280]{0:T(1024)} %param.25) | copy-start | bytes 15364
  229.1 3.6 %copy-start.9 = (f32[1280]{0:T(1024)S(1)}, f32[1280]{0:T(1024)}, u32[]{:S(2)}) copy-start(f32[1280]{0:T(1024)} %param.24) | copy-start | bytes 15364
Sparse Core Ops, SparseCore 0:
  8.9 69.1 all-gather.4
  79.7 29.2 all-gather.6
  110.5 47.8 all-gather.10
  159.8 47.8 all-gather.8
where the time goes:
time: 255 us; the launch traced here: 254 us
  waiting for transfers between devices  125 us (49%)
  matrix products  52 us (20%)
  blocking collectives  32.6 us (13%)
  local copies, waits for them, and re-layouts  24.6 us (10%)
  between operations  13.3 us (5%)
  starting transfers between devices  5.62 us (2%)
    all_gather x1, waiting for transfers between devices, shards(): lax.all_gather(w_qkv, 'dp', axis=0, tiled=True)  68.2 us
    all_to_all x1, waiting for transfers between devices, shards(): lax.all_to_all(packed, 'seq', split_axis=2, concat_axis=1, tiled=True)  53.7 us
    all_to_all x1, blocking collectives, attend_back(): lax.all_to_all(context, 'seq', split_axis=1, concat_axis=2, tiled=True)  32.6 us
    dot_general x3, matrix products, fold_rows(): return jnp.dot(left_side, shard_piece, preferred_element_type=jnp.float32)  26.2 us
    dot_general x4, matrix products, one_block(): jnp.einsum('hqk,khd->qhd', probs, value_rows, preferred_element_type=jnp....  14.2 us
    sub x4, matrix products, one_block(): weights = jnp.exp(scores - highest)  11.6 us
    reshape x2, local copies, waits for them, and re-layouts, shards(): (projected + qkv_bias).astype(jnp.bfloat16)  8.64 us
    while x2, local copies, waits for them, and re-layouts, attend_back(): context = lax.map(one_picture, packed_items)  6.55 us
  transfers between devices with their start and end apart: 5, of which 2 were waited for; matrix products, arithmetic and copies ran while one was open for 25% of the time, Pallas kernels for 0%

commit v1 on v0

v1 whole, which is shorter than its diff:
```python
import functools
import math

import jax
import jax.numpy as jnp
from jax import lax
from jax.experimental import pallas as pl
from jax.experimental.pallas import tpu as pltpu
from jax.sharding import PartitionSpec as P

HEADS = 16
HEAD_DIM = 80
LANES = 128
EPSILON = 1e-05
MESH = pl.DeviceIdType.MESH
VMEM = pl.BlockSpec(memory_space=pltpu.VMEM)


def normalize(features, gain, shift):
    average = jnp.mean(features, axis=-1, keepdims=True)
    centered = features - average
    spread = jnp.mean(centered * centered, axis=-1, keepdims=True)
    return centered * lax.rsqrt(spread + EPSILON) * gain + shift


def fold_rows(left_side, shard_piece):
    return jnp.dot(left_side, shard_piece, preferred_element_type=jnp.float32)


def ring_to_seq(place, n):
    back = place // (n // 2)
    return (1 - back) * 2 * place + back * (2 * (n - 1 - place) + 1)


def seq_to_ring(s, n):
    odd = s % 2
    return (1 - odd) * (s // 2) + odd * (n - 1 - s // 2)


def project_kernel(
    n, n_dp, x_ref, w_ref, b_ref, out_ref, buf, wbuf, tok_send, tok_recv, w_send, w_recv, f_send, f_recv
):
    d, s = lax.axis_index("dp"), lax.axis_index("seq")
    place = seq_to_ring(s, n)
    right = ring_to_seq((place + 1) % n, n)
    left = ring_to_seq((place + n - 1) % n, n)
    sibling = d + 1 - 2 * (d % 2)
    rows = x_ref.shape[0]
    half = rows // 2
    depth = w_ref.shape[0]
    images, length, _ = out_ref.shape
    tok = rows // images
    steps = n // 2
    pairs = n_dp // 2

    barrier = pltpu.get_barrier_semaphore()
    for target in (right, left):
        pl.semaphore_signal(barrier, inc=1, device_id=(d, target), device_id_type=MESH)
    for j in range(1, pairs):
        pl.semaphore_signal(barrier, inc=1, device_id=((d + 2 * j) % n_dp, s), device_id_type=MESH)
    pl.semaphore_signal(barrier, inc=1, device_id=(sibling, s), device_id_type=MESH)
    pl.semaphore_wait(barrier, 2 + pairs)

    def token_copy(way, t, h, arriving=False):
        back = t + 1 if arriving else t
        origin = (place + n - back) % n if way == 0 else (place + back) % n
        part = pl.ds(h * half, half)
        here = buf.at[origin, part]
        return pltpu.make_async_remote_copy(
            src_ref=x_ref.at[part] if (t == 0 and not arriving) else here,
            dst_ref=here,
            send_sem=tok_send.at[way, t, h],
            recv_sem=tok_recv.at[way, t, h],
            device_id=(d, right if way == 0 else left),
            device_id_type=MESH,
        )

    def slab(owner):
        return pl.ds(pl.multiple_of(owner * depth, 16), depth)

    def w_copy(j, arriving=False):
        owner = (d + n_dp - 2 * j) % n_dp if arriving else d
        return pltpu.make_async_remote_copy(
            src_ref=w_ref,
            dst_ref=wbuf.at[slab(owner)],
            send_sem=w_send.at[j],
            recv_sem=w_recv.at[j],
            device_id=((d + 2 * j) % n_dp, s),
            device_id_type=MESH,
        )

    def f_copy(j, arriving=False):
        base = sibling if arriving else d
        owner = (base + n_dp - 2 * j) % n_dp
        return pltpu.make_async_remote_copy(
            src_ref=w_ref if j == 0 else wbuf.at[slab(owner)],
            dst_ref=wbuf.at[slab(owner)],
            send_sem=f_send.at[j],
            recv_sem=f_recv.at[j],
            device_id=(sibling, s),
            device_id_type=MESH,
        )

    for j in range(1, pairs):
        w_copy(j).start()
    f_copy(0).start()
    for h in range(2):
        for way in range(2):
            token_copy(way, 0, h).start()
    wbuf[slab(d), :] = w_ref[...]

    def process(block, owner):
        y = jnp.dot(block, wbuf[...], preferred_element_type=jnp.float32) + b_ref[...]
        y = y.astype(jnp.bfloat16)
        at = pl.ds(pl.multiple_of(owner * tok, 16), tok)
        for i in range(images):
            out_ref[i, at, :] = y[i * tok : (i + 1) * tok]

    for t in range(steps):
        last = t == steps - 1
        for h in range(2):
            for way in range(2):
                if last and h != way:
                    continue
                token_copy(way, t, h, True).wait_recv()
                if t < steps - 2 or (t == steps - 2 and h == way):
                    token_copy(way, t + 1, h).start()
        if t == 0:
            for j in range(1, pairs):
                w_copy(j, True).wait_recv()
                f_copy(j).start()
            for j in range(pairs):
                f_copy(j, True).wait_recv()
            process(x_ref[...], s)
        if last:
            far = (place + n // 2) % n
            process(buf[far], ring_to_seq(far, n))
        else:

            def both(i, carry):
                origin = (place + n - (t + 1) + i * 2 * (t + 1)) % n
                process(buf[origin], ring_to_seq(origin, n))
                return carry

            lax.fori_loop(0, 2, both, 0)

    for j in range(1, pairs):
        w_copy(j).wait_send()
    for j in range(pairs):
        f_copy(j).wait_send()
    for t in range(steps):
        for h in range(2):
            for way in range(2):
                if t < steps - 1 or h == way:
                    token_copy(way, t, h).wait_send()


def project(normed, w_cols, bias, images, n, n_dp):
    rows, width = normed.shape
    depth, columns = w_cols.shape
    length = n * (rows // images)
    pairs = n_dp // 2
    dma = pltpu.SemaphoreType.DMA
    return pl.pallas_call(
        functools.partial(project_kernel, n, n_dp),
        out_shape=jax.ShapeDtypeStruct((images, length, columns), jnp.bfloat16),
        in_specs=[VMEM] * 3,
        out_specs=VMEM,
        scratch_shapes=[
            pltpu.VMEM((n, rows, width), jnp.bfloat16),
            pltpu.VMEM((width, columns), jnp.bfloat16),
            dma((2, n // 2, 2)),
            dma((2, n // 2, 2)),
            dma((pairs,)),
            dma((pairs,)),
            dma((pairs,)),
            dma((pairs,)),
        ],
        compiler_params=pltpu.CompilerParams(
            collective_id=0, has_side_effects=True, vmem_limit_bytes=40 * 1024 * 1024
        ),
        cost_estimate=pl.CostEstimate(
            flops=100 * 2 * n * rows * width * columns, bytes_accessed=n * rows * width * 2, transcendentals=0
        ),
        name="gather_project",
    )(normed, w_cols, bias)


def attend_kernel(heads, head_size, factor, packed_ref, out_ref):
    block_rows = out_ref.shape[0]
    at = pl.ds(pl.multiple_of(pl.program_id(1) * block_rows, 16), block_rows)
    mixed = []
    for h in range(heads):
        base = h * 3 * LANES
        queries = packed_ref[at, base : base + LANES]
        key_rows = packed_ref[:, base + LANES : base + 2 * LANES]
        value_rows = packed_ref[:, base + 2 * LANES : base + 3 * LANES]
        scores = lax.dot_general(
            queries, key_rows, (((1,), (1,)), ((), ())), preferred_element_type=jnp.float32
        )
        highest = jnp.max(scores, axis=-1, keepdims=True)
        weights = jnp.exp2((scores - highest) * factor).astype(jnp.bfloat16)
        summed = jnp.dot(weights, value_rows, preferred_element_type=jnp.float32)
        mixed.append(summed[:, :head_size] / summed[:, head_size : head_size + 1])
    out_ref[...] = jnp.concatenate(mixed, axis=-1).astype(jnp.bfloat16)


def attend(packed, heads, head_size):
    images, length, columns = packed.shape
    block_rows = max(r for r in range(16, 385, 16) if length % r == 0)
    factor = math.log2(math.e) / math.sqrt(head_size)
    return pl.pallas_call(
        functools.partial(attend_kernel, heads, head_size, factor),
        grid=(images, length // block_rows),
        out_shape=jax.ShapeDtypeStruct((images, length, heads * head_size), jnp.bfloat16),
        in_specs=[pl.BlockSpec((None, length, columns), lambda i, q: (i, 0, 0))],
        out_specs=pl.BlockSpec((None, block_rows, heads * head_size), lambda i, q: (i, q, 0)),
        compiler_params=pltpu.CompilerParams(vmem_limit_bytes=40 * 1024 * 1024),
        cost_estimate=pl.CostEstimate(
            flops=20 * images * heads * length * length * LANES,
            bytes_accessed=images * length * columns * 2,
            transcendentals=images * heads * length * length,
        ),
        name="attend",
    )(packed)


def exchange_kernel(n, ctx_ref, out_ref, send, recv):
    d, s = lax.axis_index("dp"), lax.axis_index("seq")
    tok = out_ref.shape[2]
    barrier = pltpu.get_barrier_semaphore()
    for t in range(1, n):
        pl.semaphore_signal(barrier, inc=1, device_id=(d, (s + t) % n), device_id_type=MESH)
    pl.semaphore_wait(barrier, n - 1)

    def rows_of(owner):
        return pl.ds(pl.multiple_of(owner * tok, 16), tok)

    def block_copy(t, arriving=False):
        peer = (s + t) % n
        slot = (s + n - t) % n if arriving else s
        return pltpu.make_async_remote_copy(
            src_ref=ctx_ref.at[:, rows_of(peer), :],
            dst_ref=out_ref.at[slot],
            send_sem=send.at[t],
            recv_sem=recv.at[t],
            device_id=(d, peer),
            device_id_type=MESH,
        )

    for t in range(1, n):
        block_copy(t).start()
    out_ref[s] = ctx_ref[:, rows_of(s), :]
    for t in range(1, n):
        block_copy(t, True).wait_recv()
    for t in range(1, n):
        block_copy(t).wait_send()


def exchange(context, n):
    images, length, columns = context.shape
    dma = pltpu.SemaphoreType.DMA
    return pl.pallas_call(
        functools.partial(exchange_kernel, n),
        out_shape=jax.ShapeDtypeStruct((n, images, length // n, columns), jnp.bfloat16),
        in_specs=[VMEM],
        out_specs=VMEM,
        scratch_shapes=[dma((n,)), dma((n,))],
        compiler_params=pltpu.CompilerParams(
            collective_id=1, has_side_effects=True, vmem_limit_bytes=16 * 1024 * 1024
        ),
        cost_estimate=pl.CostEstimate(
            flops=20_000_000_000, bytes_accessed=2 * images * length * columns, transcendentals=0
        ),
        name="exchange_context",
    )(context)


def head_columns(array, s, heads, head_size):
    span = heads * 3 * head_size
    mine = lax.dynamic_slice_in_dim(array, s * span, span, axis=1)
    mine = mine.reshape(array.shape[0], heads, 3, head_size)
    return jnp.pad(mine, ((0, 0), (0, 0), (0, 0), (0, LANES - head_size)))


def shards(
    n,
    n_dp,
    tokens,
    pre_gain,
    pre_shift,
    w_qkv,
    qkv_bias,
    w_out,
    out_bias,
    mlp_gain,
    mlp_shift,
    w_up,
    up_bias,
    w_down,
    down_bias,
):
    images_here, tok_here, width = tokens.shape
    row_count = images_here * tok_here
    heads_here = HEADS // n
    columns = heads_here * 3 * LANES
    s = lax.axis_index("seq")
    residual = tokens.reshape(row_count, width).astype(jnp.float32)
    normed = normalize(residual, pre_gain, pre_shift).astype(jnp.bfloat16)
    w_cols = head_columns(w_qkv, s, heads_here, HEAD_DIM).reshape(w_qkv.shape[0], columns)
    bias = head_columns(qkv_bias[None], s, heads_here, HEAD_DIM)
    bias = bias.at[:, :, 2, HEAD_DIM].set(1.0).reshape(1, columns)
    packed = project(normed, w_cols, bias, images_here, n, n_dp)
    context = attend(packed, heads_here, HEAD_DIM)
    context = exchange(context, n)
    context = context.transpose(1, 2, 0, 3).reshape(row_count, width)
    attended = fold_rows(context, lax.all_gather(w_out, "dp", axis=0, tiled=True))
    middle = residual + attended + out_bias
    normed_mlp = normalize(middle, mlp_gain, mlp_shift).astype(jnp.bfloat16)
    lifted = fold_rows(normed_mlp, lax.all_gather(w_up, "dp", axis=0, tiled=True))
    hidden = jax.nn.gelu(lifted + up_bias, approximate=False).astype(jnp.bfloat16)
    lowered = fold_rows(hidden, lax.all_gather(w_down, "dp", axis=0, tiled=True))
    result = (middle + lowered + down_bias).astype(jnp.bfloat16)
    return result.reshape(images_here, tok_here, width)


def solution(mesh):
    in_specs = (
        P("dp", "seq", None),
        P(),
        P(),
        P("dp", None),
        P(),
        P("dp", None),
        P(),
        P(),
        P(),
        P("dp", None),
        P(),
        P("dp", None),
        P(),
    )
    out_specs = P("dp", "seq", None)
    step = functools.partial(shards, mesh.shape["seq"], mesh.shape["dp"])
    return jax.shard_map(step, mesh=mesh, in_specs=in_specs, out_specs=out_specs, check_vma=False)
```

time: 255 us -> 171 us (0.67)
  Pallas kernels: 0 us -> 95.3 us
  waiting for transfers between devices: 125 us -> 30.8 us
  matrix products: 52 us -> 19.1 us
  blocking collectives: 32.6 us -> 0 us
  local copies, waits for them, and re-layouts: 24.6 us -> 8.53 us
  starting transfers between devices: 5.62 us -> 0.08 us
    pallas_call x0 -> x3, Pallas kernels: none -> 95.3 us  [the longest x1 63 us: project(): pl.pallas_call(functools.partial(project_kernel, n, n_dp), out_shape=jax....]
    all_gather x1 -> x0, waiting for transfers between devices: 68.2 us -> none  [shards(): lax.all_gather(w_qkv, 'dp', axis=0, tiled=True)]
    all_to_all x1 -> x0, waiting for transfers between devices: 53.7 us -> none  [shards(): lax.all_to_all(packed, 'seq', split_axis=2, concat_axis=1, tiled=True)]
    all_to_all x1 -> x0, blocking collectives: 32.6 us -> none  [attend_back(): lax.all_to_all(context, 'seq', split_axis=1, concat_axis=2, tiled=True)]
    all_gather x1, waiting for transfers between devices: 0.02 us -> 28.7 us  [shards(): lax.all_gather(w_down, 'dp', axis=0, tiled=True)]
    dot_general x4 -> x0, matrix products: 14.2 us -> none  [one_block(): jnp.einsum('hqk,khd->qhd', probs, value_rows, preferred_element_type=jnp....]
    sub x4 -> x0, matrix products: 11.6 us -> none  [one_block(): weights = jnp.exp(scores - highest)]
    reshape x5 -> x4, local copies, waits for them, and re-layouts: 10.8 us -> 3.48 us  [the longest x1 3.14 us: shards(): context = context.transpose(1, 2, 0, 3).reshape(row_count, width)]
  transfers between devices with their start and end apart: 5 -> 3, of which waited for: 2 -> 1; matrix products, arithmetic and copies ran while one was open for 25% -> 8% of each run, Pallas kernels for 0% -> 56%
where the time goes in v1:
time: 171 us
  Pallas kernels  95.3 us (56%)
  waiting for transfers between devices  30.8 us (18%)
  matrix products  19.1 us (11%)
  between operations  13.3 us (8%)
  local copies, waits for them, and re-layouts  8.53 us (5%)
  other arithmetic  3.58 us (2%)
    pallas_call x1, Pallas kernels, project(): pl.pallas_call(functools.partial(project_kernel, n, n_dp), out_shape=jax....  63 us
    all_gather x1, waiting for transfers between devices, shards(): lax.all_gather(w_down, 'dp', axis=0, tiled=True)  28.7 us
    pallas_call x1, Pallas kernels, exchange(): pl.pallas_call(functools.partial(exchange_kernel, n), out_shape=jax.Shape...  20.3 us
    dot_general x2, matrix products, fold_rows(): return jnp.dot(left_side, shard_piece, preferred_element_type=jnp.float32)  19.1 us
    pallas_call x1, Pallas kernels, attend(): pl.pallas_call(functools.partial(attend_kernel, heads, head_size, factor)...  11.9 us
  transfers between devices with their start and end apart: 3, of which 1 were waited for; matrix products, arithmetic and copies ran while one was open for 8% of the time, Pallas kernels for 56%

profile of v1, /device:TPU:0, one launch (start us, length us, event | category | flops | bytes accessed | tf_op | source)
XLA Modules:
  0.0 170.7 jit_solution(5332597332817491283)
XLA Ops:
  6.5 0.7 all-gather.4.cloned.1.call-update
  7.3 0.7 all-gather.6.cloned.1.call-update
  8.1 0.7 all-gather.8.cloned.1.call-update
  8.8 0.2 convert_reduce_fusion
  9.0 0.9 multiply_reduce_fusion.1
  9.9 0.7 div.15
  10.6 0.2 constant_dynamic-slice_fusion
  10.7 0.2 copy.17
  11.0 0.2 copy.15.w_ref
  11.3 0.8 dynamic-slice.11
  12.1 0.1 reshape.113
  12.2 0.2 scatter.4
  12.4 0.7 add_rsqrt_fusion.1
  13.2 1.5 fusion.16.x_ref
  14.6 63.0 %gather_project.1.packed_ref = bf16[2,1152,768]{2,1,0:T(8,128)(2,1)S(1)} custom-call(bf16[288,1280]{1,0:T(8,128)(2,1)S(1)} %fusion.16.x_ref, bf16[320,768]{1,0:T(8,128)(2,1)S(1)} %copy.15.w_ref, f32[1,768]{1,0:T(1,128)S(1)} %reshape.114.b_ref), custom_call_target="tpu_custom_call" | custom-call | flops 452984832000 | bytes 5898240 | tf_op jit(solution)/shard_map/gather_project/pallas_call | solution.py:164
  77.7 11.9 %attend.1.ctx_ref = bf16[2,1152,160]{2,1,0:T(8,128)(2,1)S(1)} custom-call(bf16[2,1152,768]{2,1,0:T(8,128)(2,1)S(1)} %gather_project.1.packed_ref), custom_call_target="tpu_custom_call" | custom-call | flops 13589544960 | bytes 3538944 | tf_op jit(solution)/shard_map/attend/pallas_call | solution.py:212
  89.6 20.3 %exchange_context.1 = bf16[8,2,144,160]{3,2,1,0:T(8,128)(2,1)S(1)} custom-call(bf16[2,1152,160]{2,1,0:T(8,128)(2,1)S(1)} %attend.1.ctx_ref), custom_call_target="tpu_custom_call" | custom-call | flops 20000000000 | bytes 737280 | tf_op jit(solution)/shard_map/exchange_context/pallas_call | solution.py:263
  110.0 1.7 copy.16
  111.7 3.1 %reshape.115 = bf16[288,1280]{1,0:T(8,128)(2,1)} reshape(bf16[2,144,8,160]{3,2,1,0:T(8,128)(2,1)} %copy.16) | data formatting | bytes 1474560 | tf_op jit(solution)/shard_map/reshape | solution.py:316
  114.9 3.4 %fusion.86 = (f32[288]{0:T(512)S(1)}, f32[288,1280]{1,0:T(8,128)S(1)}) fusion(f32[1280]{0:T(1024)S(1)} %copy-done.7, bf16[288,1280]{1,0:T(8,128)(2,1)} %reshape.115, bf16[1280,1280]{1,0:T(8,128)(2,1)} %all-gather.4.cloned.1.call-done, bf16[288,1280]{1,0:T(8,128)(2,1)S(1)} %bitcast.22), kind=kOutput, calls=%fused_computation.104 | convolution fusion | flops 945192704 | bytes 6232192 | tf_op jit(solution)/shard_map/dot_general | solution.py:27
  118.3 1.1 copy-done.3
  119.4 0.3 multiply_reduce_fusion
  119.7 28.7 %all-gather.8.cloned.1.call-done = bf16[2560,1280]{1,0:T(8,128)(2,1)} async-done(((bf16[640,1280]{1,0:T(8,128)(2,1)}), bf16[2560,1280]{1,0:T(8,128)(2,1)}) %all-gather.8.cloned.1.call-update) | async-done | bytes 6553616 | tf_op jit(solution)/shard_map/all_gather | solution.py:322
  148.4 15.7 %fusion.12 = bf16[288,1280]{1,0:T(8,128)(2,1)} fusion(f32[288,1280]{1,0:T(8,128)} %copy-done.3, bf16[2560,1280]{1,0:T(8,128)(2,1)} %all-gather.8.cloned.1.call-done, bf16[1280,2560]{1,0:T(8,128)(2,1)} %all-gather.6.cloned.1.call-done, f32[2560]{0:T(1024)S(1)} %copy-done.6, f32[1280]{0:T(1024)S(1)} %copy-done.8, f32[1280]{0:T(1024)S(1)} %copy-done.9, ...), kind=kOutput, calls=%fused_computation.24 | convolution fusion | flops 3826483200 | bytes 15346944 | tf_op jit(solution)/shard_map/dot_general | solution.py:27
  (34 shorter events, 0.3 us)
Async XLA Ops:
  6.5 4.0 %copy-start = (bf16[320,3840]{1,0:T(8,128)(2,1)S(1)}, bf16[320,3840]{1,0:T(8,128)(2,1)}, u32[]{:S(2)}) copy-start(bf16[320,3840]{1,0:T(8,128)(2,1)} %param.18) | copy-start | bytes 7372804
  6.5 2.2 %copy-start.1 = (bf16[2,144,1280]{2,1,0:T(8,128)(2,1)S(1)}, bf16[2,144,1280]{2,1,0:T(8,128)(2,1)}, u32[]{:S(2)}) copy-start(bf16[2,144,1280]{2,1,0:T(8,128)(2,1)} %param.15) | copy-start | bytes 2211844
  6.5 108.3 %all-gather.4.cloned.1.call-start = ((), (), s32[]{:S(2)}) async-start(), calls=%async_computation | async-start | bytes 4096000 | tf_op jit(solution)/shard_map/all_gather | solution.py:317
  7.3 112.5 %all-gather.6.cloned.1.call-start = ((), (), s32[]{:S(2)}) async-start(), calls=%async_computation.1 | async-start | bytes 8192000 | tf_op jit(solution)/shard_map/all_gather | solution.py:320
  8.0 5.2 %copy-start.4 = (f32[1280]{0:T(1024)S(1)}, f32[1280]{0:T(1024)}, u32[]{:S(2)}) copy-start(f32[1280]{0:T(1024)} %param.17) | copy-start | bytes 15364
  8.0 5.1 %copy-start.5 = (f32[1280]{0:T(1024)S(1)}, f32[1280]{0:T(1024)}, u32[]{:S(2)}) copy-start(f32[1280]{0:T(1024)} %param.16) | copy-start | bytes 15364
  8.0 140.4 %all-gather.8.cloned.1.call-start = ((), (), s32[]{:S(2)}) async-start(), calls=%async_computation.2 | async-start | bytes 8192000 | tf_op jit(solution)/shard_map/all_gather | solution.py:322
  109.9 4.9 %copy-start.2 = (bf16[2,144,1280]{2,1,0:T(8,128)(2,1)S(1)}, bf16[2,144,1280]{2,1,0:T(8,128)(2,1)}, u32[]{:S(2)}) copy-start(bf16[2,144,1280]{2,1,0:T(8,128)(2,1)} %param.15) | copy-start | bytes 2211844
  110.0 4.9 %copy-start.7 = (f32[1280]{0:T(1024)S(1)}, f32[1280]{0:T(1024)}, u32[]{:S(2)}) copy-start(f32[1280]{0:T(1024)} %param.21) | copy-start | bytes 15364
  114.8 33.6 %copy-start.6 = (f32[2560]{0:T(1024)S(1)}, f32[2560]{0:T(1024)}, u32[]{:S(2)}) copy-start(f32[2560]{0:T(1024)} %param.25) | copy-start | bytes 30724
  114.8 33.6 %copy-start.8 = (f32[1280]{0:T(1024)S(1)}, f32[1280]{0:T(1024)}, u32[]{:S(2)}) copy-start(f32[1280]{0:T(1024)} %param.27) | copy-start | bytes 15364
  114.8 33.6 %copy-start.9 = (f32[1280]{0:T(1024)S(1)}, f32[1280]{0:T(1024)}, u32[]{:S(2)}) copy-start(f32[1280]{0:T(1024)} %param.23) | copy-start | bytes 15364
  114.8 33.6 %copy-start.10 = (f32[1280]{0:T(1024)S(1)}, f32[1280]{0:T(1024)}, u32[]{:S(2)}) copy-start(f32[1280]{0:T(1024)} %param.22) | copy-start | bytes 15364
  118.3 1.1 copy-start.3
Sparse Core Ops, SparseCore 0:
  8.9 40.3 all-gather.3
  50.9 48.0 all-gather.5
  100.5 47.8 all-gather.7

commit v2 on v1

v2 whole, which is shorter than its diff:
```python
import functools
import math

import jax
import jax.numpy as jnp
from jax import lax
from jax.experimental import pallas as pl
from jax.experimental.pallas import tpu as pltpu
from jax.sharding import PartitionSpec as P

HEADS = 16
HEAD_DIM = 80
LANES = 128
EPSILON = 1e-05
MESH = pl.DeviceIdType.MESH
VMEM = pl.BlockSpec(memory_space=pltpu.VMEM)


def normalize(features, gain, shift):
    average = jnp.mean(features, axis=-1, keepdims=True)
    centered = features - average
    spread = jnp.mean(centered * centered, axis=-1, keepdims=True)
    return centered * lax.rsqrt(spread + EPSILON) * gain + shift


def fold_rows(left_side, shard_piece):
    return jnp.dot(left_side, shard_piece, preferred_element_type=jnp.float32)


def ring_to_seq(place, n):
    back = place // (n // 2)
    return (1 - back) * 2 * place + back * (2 * (n - 1 - place) + 1)


def seq_to_ring(s, n):
    odd = s % 2
    return (1 - odd) * (s // 2) + odd * (n - 1 - s // 2)


def layer_kernel(
    n,
    n_dp,
    heads,
    head_size,
    block_rows,
    x_ref,
    w_ref,
    b_ref,
    out_shard,
    up_shard,
    down_shard,
    ctx_ref,
    out_full,
    up_full,
    down_full,
    buf,
    wbuf,
    packed,
    mixed,
    landed,
    tok_send,
    tok_recv,
    w_send,
    w_recv,
    f_send,
    f_recv,
    own_sem,
    c_send,
    c_recv,
):
    d, s = lax.axis_index("dp"), lax.axis_index("seq")
    place = seq_to_ring(s, n)
    right = ring_to_seq((place + 1) % n, n)
    left = ring_to_seq((place + n - 1) % n, n)
    sibling = d + 1 - 2 * (d % 2)
    half = x_ref.shape[0] // 2
    images, length, _ = packed.shape
    tok = length // n
    steps = n // 2
    pairs = n_dp // 2
    span = heads * head_size
    shards_of = (w_ref, out_shard, up_shard, down_shard)
    wholes = (wbuf, out_full, up_full, down_full)
    factor = math.log2(math.e) / math.sqrt(head_size)

    barrier = pltpu.get_barrier_semaphore()
    for t in range(1, n):
        pl.semaphore_signal(barrier, inc=1, device_id=(d, (s + t) % n), device_id_type=MESH)
    for j in range(1, pairs):
        pl.semaphore_signal(barrier, inc=1, device_id=((d + 2 * j) % n_dp, s), device_id_type=MESH)
    pl.semaphore_signal(barrier, inc=1, device_id=(sibling, s), device_id_type=MESH)
    pl.semaphore_wait(barrier, n - 1 + pairs)

    def token_copy(way, t, h, arriving=False):
        back = t + 1 if arriving else t
        origin = (place + n - back) % n if way == 0 else (place + back) % n
        part = pl.ds(h * half, half)
        here = buf.at[origin, part]
        return pltpu.make_async_remote_copy(
            src_ref=x_ref.at[part] if (t == 0 and not arriving) else here,
            dst_ref=here,
            send_sem=tok_send.at[way, t, h],
            recv_sem=tok_recv.at[way, t, h],
            device_id=(d, right if way == 0 else left),
            device_id_type=MESH,
        )

    def slab(k, owner):
        depth = shards_of[k].shape[0]
        return pl.ds(pl.multiple_of(owner * depth, 16), depth)

    def w_copy(k, j, arriving=False):
        owner = (d + n_dp - 2 * j) % n_dp if arriving else d
        return pltpu.make_async_remote_copy(
            src_ref=shards_of[k],
            dst_ref=wholes[k].at[slab(k, owner)],
            send_sem=w_send.at[k, j],
            recv_sem=w_recv.at[k, j],
            device_id=((d + 2 * j) % n_dp, s),
            device_id_type=MESH,
        )

    def f_copy(k, j, arriving=False):
        base = sibling if arriving else d
        owner = (base + n_dp - 2 * j) % n_dp
        there = wholes[k].at[slab(k, owner)]
        return pltpu.make_async_remote_copy(
            src_ref=shards_of[k] if j == 0 else there,
            dst_ref=there,
            send_sem=f_send.at[k, j],
            recv_sem=f_recv.at[k, j],
            device_id=(sibling, s),
            device_id_type=MESH,
        )

    def pass_on(k):
        for j in range(1, pairs):
            w_copy(k, j, True).wait_recv()
            f_copy(k, j).start()

    def own_copy(k):
        return pltpu.make_async_copy(shards_of[k], wholes[k].at[slab(k, d)], own_sem.at[k])

    def rows_of(owner):
        return pl.ds(pl.multiple_of(owner * tok, 16), tok)

    def ctx_copy(i, t, arriving=False):
        peer = (s + t) % n
        slot = (s + n - t) % n if arriving else s
        return pltpu.make_async_remote_copy(
            src_ref=mixed.at[i, rows_of(peer), :],
            dst_ref=landed.at[slot, i],
            send_sem=c_send.at[i, t],
            recv_sem=c_recv.at[i, t],
            device_id=(d, peer),
            device_id_type=MESH,
        )

    for j in range(1, pairs):
        w_copy(0, j).start()
    f_copy(0, 0).start()
    for h in range(2):
        for way in range(2):
            token_copy(way, 0, h).start()
    for k in range(1, 4):
        for j in range(1, pairs):
            w_copy(k, j).start()
        f_copy(k, 0).start()
        own_copy(k).start()
    wbuf[slab(0, d), :] = w_ref[...]

    def process(block, owner):
        y = jnp.dot(block, wbuf[...], preferred_element_type=jnp.float32) + b_ref[...]
        y = y.astype(jnp.bfloat16)
        for i in range(images):
            packed[i, rows_of(owner), :] = y[i * tok : (i + 1) * tok]

    for t in range(steps):
        last = t == steps - 1
        for h in range(2):
            for way in range(2):
                if last and h != way:
                    continue
                token_copy(way, t, h, True).wait_recv()
                if t < steps - 2 or (t == steps - 2 and h == way):
                    token_copy(way, t + 1, h).start()
        if t == 0:
            pass_on(0)
            for j in range(pairs):
                f_copy(0, j, True).wait_recv()
            process(x_ref[...], s)
        if last:
            pass_on(1)
            far = (place + n // 2) % n
            process(buf[far], ring_to_seq(far, n))
        else:

            def both(i, carry):
                origin = (place + n - (t + 1) + i * 2 * (t + 1)) % n
                process(buf[origin], ring_to_seq(origin, n))
                return carry

            lax.fori_loop(0, 2, both, 0)

    def attend_image(i, carry):
        def attend_block(block, inner):
            at = pl.ds(pl.multiple_of(block * block_rows, 16), block_rows)
            parts = []
            for h in range(heads):
                base = h * 3 * LANES
                queries = packed[i, at, base : base + LANES]
                key_rows = packed[i, :, base + LANES : base + 2 * LANES]
                value_rows = packed[i, :, base + 2 * LANES : base + 3 * LANES]
                scores = lax.dot_general(
                    queries, key_rows, (((1,), (1,)), ((), ())), preferred_element_type=jnp.float32
                )
                highest = jnp.max(scores, axis=-1, keepdims=True)
                weights = jnp.exp2((scores - highest) * factor).astype(jnp.bfloat16)
                summed = jnp.dot(weights, value_rows, preferred_element_type=jnp.float32)
                parts.append(summed[:, :head_size] / summed[:, head_size : head_size + 1])
            mixed[i, at, :] = jnp.concatenate(parts, axis=-1).astype(jnp.bfloat16)
            return inner

        lax.fori_loop(0, length // block_rows, attend_block, 0)
        landed[s, i] = mixed[i, rows_of(s), :]
        for t in range(1, n):
            ctx_copy(i, t).start()
        return carry

    lax.fori_loop(0, images, attend_image, 0)
    pass_on(2)

    def gather_image(i, carry):
        for t in range(1, n):
            ctx_copy(i, t, True).wait_recv()
        rows = pl.ds(pl.multiple_of(i * tok, 16), tok)
        for owner in range(n):
            ctx_ref[rows, owner * span : (owner + 1) * span] = landed[owner, i]
        return carry

    lax.fori_loop(0, images, gather_image, 0)
    pass_on(3)

    for k in range(4):
        for j in range(pairs):
            if k > 0:
                f_copy(k, j, True).wait_recv()
            if j > 0:
                w_copy(k, j).wait_send()
            f_copy(k, j).wait_send()
        if k > 0:
            own_copy(k).wait()
    for t in range(steps):
        for h in range(2):
            for way in range(2):
                if t < steps - 1 or h == way:
                    token_copy(way, t, h).wait_send()
    for i in range(images):
        for t in range(1, n):
            ctx_copy(i, t).wait_send()


def attention_and_weights(normed, w_cols, bias, w_out, w_up, w_down, images, heads, n, n_dp):
    rows, width = normed.shape
    columns = w_cols.shape[1]
    tok = rows // images
    length = n * tok
    pairs = n_dp // 2
    span = heads * HEAD_DIM
    block_rows = max(r for r in range(16, 385, 16) if length % r == 0)
    dma = pltpu.SemaphoreType.DMA
    half = jnp.bfloat16
    anywhere = pl.BlockSpec(memory_space=pl.ANY)

    def full(shard):
        return jax.ShapeDtypeStruct((n_dp * shard.shape[0], shard.shape[1]), half)

    return pl.pallas_call(
        functools.partial(layer_kernel, n, n_dp, heads, HEAD_DIM, block_rows),
        out_shape=(jax.ShapeDtypeStruct((rows, n * span), half), full(w_out), full(w_up), full(w_down)),
        in_specs=[VMEM] * 6,
        out_specs=(VMEM, anywhere, anywhere, anywhere),
        scratch_shapes=[
            pltpu.VMEM((n, rows, width), half),
            pltpu.VMEM((width, columns), half),
            pltpu.VMEM((images, length, columns), half),
            pltpu.VMEM((images, length, span), half),
            pltpu.VMEM((n, images, tok, span), half),
            dma((2, n // 2, 2)),
            dma((2, n // 2, 2)),
            dma((4, pairs)),
            dma((4, pairs)),
            dma((4, pairs)),
            dma((4, pairs)),
            dma((4,)),
            dma((images, n)),
            dma((images, n)),
        ],
        compiler_params=pltpu.CompilerParams(
            collective_id=0, has_side_effects=True, vmem_limit_bytes=56 * 1024 * 1024
        ),
        name="attention_and_weights",
    )(normed, w_cols, bias, w_out, w_up, w_down)


def head_columns(array, s, heads, head_size):
    span = heads * 3 * head_size
    mine = lax.dynamic_slice_in_dim(array, s * span, span, axis=1)
    mine = mine.reshape(array.shape[0], heads, 3, head_size)
    return jnp.pad(mine, ((0, 0), (0, 0), (0, 0), (0, LANES - head_size)))


def shards(
    n,
    n_dp,
    tokens,
    pre_gain,
    pre_shift,
    w_qkv,
    qkv_bias,
    w_out,
    out_bias,
    mlp_gain,
    mlp_shift,
    w_up,
    up_bias,
    w_down,
    down_bias,
):
    images_here, tok_here, width = tokens.shape
    row_count = images_here * tok_here
    heads_here = HEADS // n
    columns = heads_here * 3 * LANES
    s = lax.axis_index("seq")
    residual = tokens.reshape(row_count, width).astype(jnp.float32)
    normed = normalize(residual, pre_gain, pre_shift).astype(jnp.bfloat16)
    w_cols = head_columns(w_qkv, s, heads_here, HEAD_DIM).reshape(w_qkv.shape[0], columns)
    bias = head_columns(qkv_bias[None], s, heads_here, HEAD_DIM)
    bias = bias.at[:, :, 2, HEAD_DIM].set(1.0).reshape(1, columns)
    context, w_out, w_up, w_down = attention_and_weights(
        normed, w_cols, bias, w_out, w_up, w_down, images_here, heads_here, n, n_dp
    )
    attended = fold_rows(context, w_out)
    middle = residual + attended + out_bias
    normed_mlp = normalize(middle, mlp_gain, mlp_shift).astype(jnp.bfloat16)
    lifted = fold_rows(normed_mlp, w_up)
    hidden = jax.nn.gelu(lifted + up_bias, approximate=False).astype(jnp.bfloat16)
    lowered = fold_rows(hidden, w_down)
    result = (middle + lowered + down_bias).astype(jnp.bfloat16)
    return result.reshape(images_here, tok_here, width)


def solution(mesh):
    in_specs = (
        P("dp", "seq", None),
        P(),
        P(),
        P("dp", None),
        P(),
        P("dp", None),
        P(),
        P(),
        P(),
        P("dp", None),
        P(),
        P("dp", None),
        P(),
    )
    out_specs = P("dp", "seq", None)
    step = functools.partial(shards, mesh.shape["seq"], mesh.shape["dp"])
    return jax.shard_map(step, mesh=mesh, in_specs=in_specs, out_specs=out_specs, check_vma=False)
```

time: 171 us -> 146 us (0.85)
  waiting for transfers between devices: 30.8 us -> 0 us
  Pallas kernels: 95.3 us -> 114 us
  between operations: 13.3 us -> 0.14 us
    all_gather x3 -> x0, waiting for transfers between devices: 28.7 us -> none  [the longest x1 28.7 us: shards(): lax.all_gather(w_down, 'dp', axis=0, tiled=True)]
    pallas_call x3 -> x1, Pallas kernels: 95.3 us -> 114 us  [attention_and_weights(): pl.pallas_call(functools.partial(layer_kernel, n, n_dp, heads, HEAD_DIM,...]
    reshape x1 -> x0, local copies, waits for them, and re-layouts: 3.14 us -> none  [shards(): context = context.transpose(1, 2, 0, 3).reshape(row_count, width)]
    unnamed x3 -> x0, waiting for transfers between devices: 2.09 us -> none
    reshape x1, local copies, waits for them, and re-layouts: 0.24 us -> 2.08 us  [shards(): head_columns(w_qkv, s, heads_here, HEAD_DIM)]
    pad x2, local copies, waits for them, and re-layouts: 0.07 us -> 1.87 us  [head_columns(): return jnp.pad(mine, ((0, 0), (0, 0), (0, 0), (0, LANES - head_size)))]
  transfers between devices with their start and end apart: 3 -> 0, of which waited for: 1 -> 0; matrix products, arithmetic and copies ran while one was open for 8% -> 0% of each run, Pallas kernels for 56% -> 0%
where the time goes in v2:
time: 146 us
  Pallas kernels  114 us (78%)
  matrix products  19.1 us (13%)
  local copies, waits for them, and re-layouts  8.2 us (6%)
  other arithmetic  4.28 us (3%)
    pallas_call x1, Pallas kernels, attention_and_weights(): pl.pallas_call(functools.partial(layer_kernel, n, n_dp, heads, HEAD_DIM,...  114 us
    dot_general x2, matrix products, fold_rows(): return jnp.dot(left_side, shard_piece, preferred_element_type=jnp.float32)  19.1 us

profile of v2, /device:TPU:0, one launch (start us, length us, event | category | flops | bytes accessed | tf_op | source)
XLA Modules:
  0.0 145.9 jit_solution(17482610392252898250)
XLA Ops:
  0.0 0.0 copy-start
  0.0 0.9 dynamic-slice.11
  0.9 0.1 reshape.110
  1.0 0.2 scatter.4
  1.2 0.6 reshape.111.b_ref
  1.9 1.3 convert_reduce_fusion
  3.2 1.5 multiply_reduce_fusion.1
  4.6 0.1 div.15
  4.7 0.1 rsqrt.20
  4.8 0.2 constant_dynamic-slice_fusion
  5.0 0.9 copy.16
  5.9 1.9 %pad.12 = bf16[320,2,3,128]{0,3,2,1:T(8,128)(2,1)} pad(bf16[320,2,3,80]{0,3,2,1:T(8,128)(2,1)} %bitcast.20, bf16[]{:T(256)} %constant.84.clone.1), padding=0_0x0_0x0_0x0_48 | pad | bytes 798722 | tf_op jit(solution)/shard_map/jit(_pad)/pad | solution.py:310
  7.8 2.1 %copy.15.w_ref = bf16[320,768]{1,0:T(8,128)(2,1)} copy(bf16[320,768]{0,1:T(8,128)(2,1)} %bitcast.19) | data formatting | bytes 983040 | tf_op jit(solution)/shard_map/reshape | solution.py:337
  9.9 0.0 copy-done.3
  9.9 1.2 fusion.16.x_ref
  11.1 114.2 %attention_and_weights.1 = (bf16[288,1280]{1,0:T(8,128)(2,1)}, bf16[1280,1280]{1,0:T(8,128)(2,1)}, bf16[1280,2560]{1,0:T(8,128)(2,1)}, bf16[2560,1280]{1,0:T(8,128)(2,1)}) custom-call(bf16[288,1280]{1,0:T(8,128)(2,1)} %fusion.16.x_ref, bf16[320,768]{1,0:T(8,128)(2,1)} %copy.15.w_ref, f32[1,768]{1,0:T(1,128)} %reshape.111.b_ref, bf16[320,1280]{1,0:T(8,128)(2,1)} %out_shard.1, ...), custom_call_target="tpu_custom_call" | custom-call | tf_op jit(solution)/shard_map/attention_and_weights/pallas_call | solution.py:278
  125.3 0.0 copy-start.5
  125.3 0.0 copy-start.7
  125.3 0.0 copy-start.8
  125.3 0.0 copy-start.9
  125.3 3.4 %fusion.86 = (f32[288]{0:T(512)S(1)}, f32[288,1280]{1,0:T(8,128)S(1)}) fusion(f32[1280]{0:T(1024)S(1)} %copy-done.6, bf16[288,1280]{1,0:T(8,128)(2,1)} %get-tuple-element.21, bf16[1280,1280]{1,0:T(8,128)(2,1)} %get-tuple-element.22, bf16[288,1280]{1,0:T(8,128)(2,1)S(1)} %bitcast.18), kind=kOutput, calls=%fused_computation.104 | convolution fusion | flops 945192704 | bytes 6232192 | tf_op jit(solution)/shard_map/dot_general | solution.py:27
  128.7 1.1 copy-done.2
  129.9 0.3 multiply_reduce_fusion
  130.2 15.7 %fusion.12 = bf16[288,1280]{1,0:T(8,128)(2,1)} fusion(f32[288,1280]{1,0:T(8,128)} %copy-done.2, bf16[2560,1280]{1,0:T(8,128)(2,1)} %get-tuple-element.24, bf16[1280,2560]{1,0:T(8,128)(2,1)} %get-tuple-element.23, f32[2560]{0:T(1024)S(1)} %copy-done.5, f32[1280]{0:T(1024)S(1)} %copy-done.7, f32[1280]{0:T(1024)S(1)} %copy-done.8, f32[1280]{0:T(1024)S(1)} %copy-done.9, ...), kind=kOutput, calls=%fused_computation.24 | convolution fusion | flops 3826483200 | bytes 15346944 | tf_op jit(solution)/shard_map/dot_general | solution.py:27
  (19 shorter events, 0.1 us)
Async XLA Ops:
  0.0 4.8 %copy-start = (bf16[320,3840]{1,0:T(8,128)(2,1)S(1)}, bf16[320,3840]{1,0:T(8,128)(2,1)}, u32[]{:S(2)}) copy-start(bf16[320,3840]{1,0:T(8,128)(2,1)} %param.18) | copy-start | bytes 7372804
  0.0 9.8 %copy-start.1 = (bf16[2,144,1280]{2,1,0:T(8,128)(2,1)S(1)}, bf16[2,144,1280]{2,1,0:T(8,128)(2,1)}, u32[]{:S(2)}) copy-start(bf16[2,144,1280]{2,1,0:T(8,128)(2,1)} %param.15) | copy-start | bytes 2211844
  0.0 9.8 %copy-start.3 = (f32[1280]{0:T(1024)S(1)}, f32[1280]{0:T(1024)}, u32[]{:S(2)}) copy-start(f32[1280]{0:T(1024)} %param.17) | copy-start | bytes 15364
  0.0 9.8 %copy-start.4 = (f32[1280]{0:T(1024)S(1)}, f32[1280]{0:T(1024)}, u32[]{:S(2)}) copy-start(f32[1280]{0:T(1024)} %param.16) | copy-start | bytes 15364
  11.1 114.2 %copy-start.6 = (f32[1280]{0:T(1024)S(1)}, f32[1280]{0:T(1024)}, u32[]{:S(2)}) copy-start(f32[1280]{0:T(1024)} %param.21) | copy-start | bytes 15364
  125.3 4.9 %copy-start.5 = (f32[2560]{0:T(1024)S(1)}, f32[2560]{0:T(1024)}, u32[]{:S(2)}) copy-start(f32[2560]{0:T(1024)} %param.25) | copy-start | bytes 30724
  125.3 4.9 %copy-start.7 = (f32[1280]{0:T(1024)S(1)}, f32[1280]{0:T(1024)}, u32[]{:S(2)}) copy-start(f32[1280]{0:T(1024)} %param.27) | copy-start | bytes 15364
  125.3 4.9 %copy-start.8 = (f32[1280]{0:T(1024)S(1)}, f32[1280]{0:T(1024)}, u32[]{:S(2)}) copy-start(f32[1280]{0:T(1024)} %param.23) | copy-start | bytes 15364
  125.3 4.9 %copy-start.9 = (f32[1280]{0:T(1024)S(1)}, f32[1280]{0:T(1024)}, u32[]{:S(2)}) copy-start(f32[1280]{0:T(1024)} %param.22) | copy-start | bytes 15364
  128.7 1.1 copy-start.2

commit v3 on v2

--- a/solution.py
+++ b/solution.py
@@ -49,11 +49,19 @@
     out_shard,
     up_shard,
     down_shard,
-    ctx_ref,
+    tok_ref,
+    ob_ref,
+    gain_ref,
+    shift_ref,
+    ub_ref,
+    middle_ref,
+    hidden_ref,
+    down_full,
     out_full,
     up_full,
-    down_full,
+    ctx_ref,
     buf,
+    wraw,
     wbuf,
     packed,
     mixed,
@@ -80,7 +88,7 @@
     pairs = n_dp // 2
     span = heads * head_size
     shards_of = (w_ref, out_shard, up_shard, down_shard)
-    wholes = (wbuf, out_full, up_full, down_full)
+    wholes = (wraw, out_full, up_full, down_full)
     factor = math.log2(math.e) / math.sqrt(head_size)
 
     barrier = pltpu.get_barrier_semaphore()
@@ -166,8 +174,9 @@
         for j in range(1, pairs):
             w_copy(k, j).start()
         f_copy(k, 0).start()
-        own_copy(k).start()
-    wbuf[slab(0, d), :] = w_ref[...]
+    own_copy(3).start()
+    for k in range(3):
+        wholes[k][slab(k, d), :] = shards_of[k][...]
 
     def process(block, owner):
         y = jnp.dot(block, wbuf[...], preferred_element_type=jnp.float32) + b_ref[...]
@@ -188,6 +197,9 @@
             pass_on(0)
             for j in range(pairs):
                 f_copy(0, j, True).wait_recv()
+            wbuf[...] = jnp.zeros_like(wbuf)
+            for g in range(3 * heads):
+                wbuf[:, g * LANES : g * LANES + head_size] = wraw[:, g * head_size : (g + 1) * head_size]
             process(x_ref[...], s)
         if last:
             pass_on(1)
@@ -238,18 +250,41 @@
             ctx_ref[rows, owner * span : (owner + 1) * span] = landed[owner, i]
         return carry
 
+    for k in range(1, 3):
+        for j in range(pairs):
+            f_copy(k, j, True).wait_recv()
     lax.fori_loop(0, images, gather_image, 0)
+
+    def tile_of(c):
+        return pl.ds(pl.multiple_of(c * 2 * LANES, 2 * LANES), 2 * LANES)
+
+    def out_tile(c, carry):
+        cols = tile_of(c)
+        attended = jnp.dot(ctx_ref[...], out_full[:, cols], preferred_element_type=jnp.float32)
+        middle_ref[:, cols] = tok_ref[:, cols].astype(jnp.float32) + attended + ob_ref[:, cols]
+        return carry
+
+    def up_tile(c, carry):
+        cols = tile_of(c)
+        lifted = jnp.dot(ctx_ref[...], up_full[:, cols], preferred_element_type=jnp.float32)
+        lifted = lifted + ub_ref[:, cols]
+        hidden = 0.5 * lifted * (1.0 + lax.erf(lifted * math.sqrt(0.5)))
+        hidden_ref[:, cols] = hidden.astype(jnp.bfloat16)
+        return carry
+
+    lax.fori_loop(0, out_full.shape[1] // (2 * LANES), out_tile, 0)
+    ctx_ref[...] = normalize(middle_ref[...], gain_ref[...], shift_ref[...]).astype(jnp.bfloat16)
+    lax.fori_loop(0, up_full.shape[1] // (2 * LANES), up_tile, 0)
     pass_on(3)
 
     for k in range(4):
         for j in range(pairs):
-            if k > 0:
+            if k == 3:
                 f_copy(k, j, True).wait_recv()
             if j > 0:
                 w_copy(k, j).wait_send()
             f_copy(k, j).wait_send()
-        if k > 0:
-            own_copy(k).wait()
+    own_copy(3).wait()
     for t in range(steps):
         for h in range(2):
             for way in range(2):
@@ -260,9 +295,11 @@
             ctx_copy(i, t).wait_send()
 
 
-def attention_and_weights(normed, w_cols, bias, w_out, w_up, w_down, images, heads, n, n_dp):
+def layer_until_hidden(
+    normed, w_cols, bias, w_out, w_up, w_down, tokens, out_bias, gain, shift, up_bias, images, heads, n, n_dp
+):
     rows, width = normed.shape
-    columns = w_cols.shape[1]
+    columns = 3 * heads * LANES
     tok = rows // images
     length = n * tok
     pairs = n_dp // 2
@@ -273,15 +310,23 @@
     anywhere = pl.BlockSpec(memory_space=pl.ANY)
 
     def full(shard):
-        return jax.ShapeDtypeStruct((n_dp * shard.shape[0], shard.shape[1]), half)
+        return (n_dp * shard.shape[0], shard.shape[1])
 
     return pl.pallas_call(
         functools.partial(layer_kernel, n, n_dp, heads, HEAD_DIM, block_rows),
-        out_shape=(jax.ShapeDtypeStruct((rows, n * span), half), full(w_out), full(w_up), full(w_down)),
-        in_specs=[VMEM] * 6,
-        out_specs=(VMEM, anywhere, anywhere, anywhere),
+        out_shape=(
+            jax.ShapeDtypeStruct((rows, width), jnp.float32),
+            jax.ShapeDtypeStruct((rows, w_up.shape[1]), half),
+            jax.ShapeDtypeStruct(full(w_down), half),
+        ),
+        in_specs=[VMEM] * 11,
+        out_specs=(VMEM, VMEM, anywhere),
         scratch_shapes=[
+            pltpu.VMEM(full(w_out), half),
+            pltpu.VMEM(full(w_up), half),
+            pltpu.VMEM((rows, n * span), half),
             pltpu.VMEM((n, rows, width), half),
+            pltpu.VMEM(full(w_cols), half),
             pltpu.VMEM((width, columns), half),
             pltpu.VMEM((images, length, columns), half),
             pltpu.VMEM((images, length, span), half),
@@ -299,8 +344,8 @@
         compiler_params=pltpu.CompilerParams(
             collective_id=0, has_side_effects=True, vmem_limit_bytes=56 * 1024 * 1024
         ),
-        name="attention_and_weights",
-    )(normed, w_cols, bias, w_out, w_up, w_down)
+        name="layer_until_hidden",
+    )(normed, w_cols, bias, w_out, w_up, w_down, tokens, out_bias, gain, shift, up_bias)
 
 
 def head_columns(array, s, heads, head_size):
@@ -334,17 +379,27 @@
     s = lax.axis_index("seq")
     residual = tokens.reshape(row_count, width).astype(jnp.float32)
     normed = normalize(residual, pre_gain, pre_shift).astype(jnp.bfloat16)
-    w_cols = head_columns(w_qkv, s, heads_here, HEAD_DIM).reshape(w_qkv.shape[0], columns)
+    span = heads_here * 3 * HEAD_DIM
+    w_cols = lax.dynamic_slice_in_dim(w_qkv, s * span, span, axis=1)
     bias = head_columns(qkv_bias[None], s, heads_here, HEAD_DIM)
     bias = bias.at[:, :, 2, HEAD_DIM].set(1.0).reshape(1, columns)
-    context, w_out, w_up, w_down = attention_and_weights(
-        normed, w_cols, bias, w_out, w_up, w_down, images_here, heads_here, n, n_dp
+    middle, hidden, w_down = layer_until_hidden(
+        normed,
+        w_cols,
+        bias,
+        w_out,
+        w_up,
+        w_down,
+        tokens.reshape(row_count, width),
+        out_bias[None],
+        mlp_gain[None],
+        mlp_shift[None],
+        up_bias[None],
+        images_here,
+        heads_here,
+        n,
+        n_dp,
     )
-    attended = fold_rows(context, w_out)
-    middle = residual + attended + out_bias
-    normed_mlp = normalize(middle, mlp_gain, mlp_shift).astype(jnp.bfloat16)
-    lifted = fold_rows(normed_mlp, w_up)
-    hidden = jax.nn.gelu(lifted + up_bias, approximate=False).astype(jnp.bfloat16)
     lowered = fold_rows(hidden, w_down)
     result = (middle + lowered + down_bias).astype(jnp.bfloat16)
     return result.reshape(images_here, tok_here, width)

time: 146 us -> 128 us (0.88)
  matrix products: 19.1 us -> 6.6 us
  local copies, waits for them, and re-layouts: 8.2 us -> 5.32 us
  Pallas kernels: 114 us -> 112 us
    dot_general x2 -> x1, matrix products: 19.1 us -> 6.6 us  [fold_rows(): return jnp.dot(left_side, shard_piece, preferred_element_type=jnp.float32)]
    pallas_call x1, Pallas kernels: 114 us -> 112 us  [layer_until_hidden(): pl.pallas_call(functools.partial(layer_kernel, n, n_dp, heads, HEAD_DIM,...]
    broadcast_in_dim x0 -> x4, local copies, waits for them, and re-layouts: none -> 2.4 us  [the longest x1 0.61 us: shards(): out_bias[None]]
    reshape x1 -> x0, local copies, waits for them, and re-layouts: 2.08 us -> none  [shards(): head_columns(w_qkv, s, heads_here, HEAD_DIM)]
    unnamed x21 -> x18, local copies, waits for them, and re-layouts: 2.09 us -> 0.04 us
    pad x2 -> x1, local copies, waits for them, and re-layouts: 1.87 us -> 0.01 us  [head_columns(): return jnp.pad(mine, ((0, 0), (0, 0), (0, 0), (0, LANES - head_size)))]
where the time goes in v3:
time: 128 us
  Pallas kernels  112 us (88%)
  matrix products  6.6 us (5%)
  local copies, waits for them, and re-layouts  5.32 us (4%)
  other arithmetic  3.98 us (3%)
    pallas_call x1, Pallas kernels, layer_until_hidden(): pl.pallas_call(functools.partial(layer_kernel, n, n_dp, heads, HEAD_DIM,...  112 us
    dot_general x1, matrix products, fold_rows(): return jnp.dot(left_side, shard_piece, preferred_element_type=jnp.float32)  6.6 us

profile of v3, /device:TPU:0, one launch (start us, length us, event | category | flops | bytes accessed | tf_op | source)
XLA Modules:
  0.0 127.6 jit_solution(6858103235232972324)
XLA Ops:
  0.0 0.0 copy-start
  0.0 0.0 copy-start.6
  0.0 0.0 copy-start.5
  0.0 0.0 copy-start.3
  0.1 0.9 dynamic-slice.11
  1.0 0.1 reshape.88
  1.1 0.2 scatter.4
  1.3 0.6 reshape.89.b_ref
  1.9 1.3 %convert_reduce_fusion = f32[2,144]{1,0:T(2,128)S(1)} fusion(bf16[2,144,1280]{2,1,0:T(8,128)(2,1)} %param.15), kind=kLoop, calls=%fused_computation.4 | loop fusion | flops 736992 | bytes 738432 | tf_op jit(solution)/shard_map/reduce_sum | solution.py:20
  3.2 1.5 %fusion.3 = f32[2,144]{1,0:T(2,128)S(1)} fusion(bf16[2,144,1280]{2,1,0:T(8,128)(2,1)} %param.15, f32[2,144]{1,0:T(2,128)S(1)} %broadcast_multiply_fusion), kind=kLoop, calls=%fused_computation.6 | loop fusion | flops 1474272 | bytes 739584 | tf_op jit(solution)/shard_map/reduce_sum | solution.py:22
  4.6 0.1 div.9
  4.7 0.1 rsqrt.12
  4.8 0.0 copy-done.5
  4.8 0.6 broadcast_in_dim.8.ob_ref
  5.4 0.6 broadcast_in_dim.9.gain_ref
  6.0 0.6 broadcast_in_dim.20.shift_ref
  6.6 0.0 copy-done.2
  6.6 0.6 broadcast_in_dim.21.ub_ref
  7.2 0.0 copy-done
  7.2 0.9 constant_dynamic-slice_fusion.w_ref
  8.1 0.0 copy-done.1
  8.1 1.2 add_convert_fusion.x_ref
  9.4 111.6 %layer_until_hidden.1 = (f32[288,1280]{1,0:T(8,128)}, bf16[288,2560]{1,0:T(8,128)(2,1)}, bf16[2560,1280]{1,0:T(8,128)(2,1)}) custom-call(bf16[288,1280]{1,0:T(8,128)(2,1)} %add_convert_fusion.x_ref, bf16[320,480]{1,0:T(8,128)(2,1)} %constant_dynamic-slice_fusion.w_ref, f32[1,768]{1,0:T(1,128)} %reshape.89.b_ref, bf16[320,1280]{1,0:T(8,128)(2,1)} %out_shard.1, ...), custom_call_target="tpu_custom_call" | custom-call | tf_op jit(solution)/shard_map/layer_until_hidden/pallas_call | solution.py:315
  121.0 6.6 %fusion.1 = bf16[288,1280]{1,0:T(8,128)(2,1)} fusion(f32[288,1280]{1,0:T(8,128)} %get-tuple-element.20, bf16[288,2560]{1,0:T(8,128)(2,1)} %get-tuple-element.21, bf16[2560,1280]{1,0:T(8,128)(2,1)} %get-tuple-element.22, f32[1280]{0:T(1024)S(1)} %copy-done.8), kind=kOutput, calls=%fused_computation.2 | convolution fusion | flops 1888542720 | bytes 10245120 | tf_op jit(solution)/shard_map/dot_general | solution.py:27
  (14 shorter events, 0.0 us)
Async XLA Ops:
  0.0 7.2 %copy-start = (bf16[320,3840]{1,0:T(8,128)(2,1)S(1)}, bf16[320,3840]{1,0:T(8,128)(2,1)}, u32[]{:S(2)}) copy-start(bf16[320,3840]{1,0:T(8,128)(2,1)} %param.18) | copy-start | bytes 7372804
  0.0 8.1 %copy-start.1 = (bf16[2,144,1280]{2,1,0:T(8,128)(2,1)S(1)}, bf16[2,144,1280]{2,1,0:T(8,128)(2,1)}, u32[]{:S(2)}) copy-start(bf16[2,144,1280]{2,1,0:T(8,128)(2,1)} %param.15) | copy-start | bytes 2211844
  0.0 6.6 %copy-start.2 = (f32[2560]{0:T(1024)S(1)}, f32[2560]{0:T(1024)}, u32[]{:S(2)}) copy-start(f32[2560]{0:T(1024)} %param.25) | copy-start | bytes 30724
  0.0 6.0 %copy-start.7 = (f32[1280]{0:T(1024)S(1)}, f32[1280]{0:T(1024)}, u32[]{:S(2)}) copy-start(f32[1280]{0:T(1024)} %param.23) | copy-start | bytes 15364
  0.0 5.4 %copy-start.6 = (f32[1280]{0:T(1024)S(1)}, f32[1280]{0:T(1024)}, u32[]{:S(2)}) copy-start(f32[1280]{0:T(1024)} %param.22) | copy-start | bytes 15364
  0.0 4.8 %copy-start.5 = (f32[1280]{0:T(1024)S(1)}, f32[1280]{0:T(1024)}, u32[]{:S(2)}) copy-start(f32[1280]{0:T(1024)} %param.21) | copy-start | bytes 15364
  0.0 8.1 %copy-start.3 = (f32[1280]{0:T(1024)S(1)}, f32[1280]{0:T(1024)}, u32[]{:S(2)}) copy-start(f32[1280]{0:T(1024)} %param.17) | copy-start | bytes 15364
  0.0 8.1 %copy-start.4 = (f32[1280]{0:T(1024)S(1)}, f32[1280]{0:T(1024)}, u32[]{:S(2)}) copy-start(f32[1280]{0:T(1024)} %param.16) | copy-start | bytes 15364
  9.4 111.6 %copy-start.8 = (f32[1280]{0:T(1024)S(1)}, f32[1280]{0:T(1024)}, u32[]{:S(2)}) copy-start(f32[1280]{0:T(1024)} %param.27) | copy-start | bytes 15364
